TPU v7x, 32 devices: a whole 2x2x4 slice. The times are simulated.
32 devices in a mesh: cp: 16 (over z, x, core), tp: 2 (over y).
Axes of the slice: x: 2, y: 2, z: 4, core: 2. Of those that a mesh axis runs over, the one named last changes fastest.
Arguments:
- hidden: bfloat16 [8192, 4096], P('cp', 'tp'), may hold values from -6 to 6
- norm_gain: float32 [4096], replicated, may hold values from 0.5 to 1.5
- w_query: bfloat16 [4096, 4096], P(None, 'tp'), may hold values from -0.140625 to 0.140625
- w_key: bfloat16 [4096, 1024], P(None, 'tp'), may hold values from -4 to 4
- w_value: bfloat16 [4096, 1024], P(None, 'tp'), may hold values from -0.09375 to 0.09375
- w_out: bfloat16 [4096, 4096], P('tp'), may hold values from -0.5 to 0.5
- doc_ids: int32 [8192], P('cp'), may hold values from 0 to 5, never falling along the last dimension, each value on 1 to 6144 neighbouring positions
Outputs:
- updated: bfloat16 [8192, 4096], P('cp', 'tp')
Inputs may be any that keep to these rules, and one draw needn't show every extreme that they name: `doc_ids`: document numbers never fall along the sequence; every document has 1 to 6144 tokens.
All inputs are finite; a program needn't handle non-finite values.
Results may differ from a plain program's by a relative error of at most 0.017.
The roundings to bfloat16 on the way count: a program that leaves them out, or rounds other values in their place, can miss the bound.
Values may be sent and summed in bfloat16 or wider, within the bound.
A program may use at most 128 MiB of HBM per device.

v0:
```python
import jax
import jax.numpy as jnp
from jax import lax
from jax.sharding import PartitionSpec as P

HEADS = 32
KV_HEADS = 8
HEAD_SIZE = 128
epsilon = 1e-05
rope_base = 500000.0


def rotate(vectors, positions):
    half = HEAD_SIZE // 2
    freqs = rope_base ** (-jnp.arange(half, dtype=jnp.float32) * 2.0 / HEAD_SIZE)
    angles = positions.astype(jnp.float32)[:, None] * freqs[None, :]
    cosine = jnp.cos(angles)[:, None, :]
    sine = jnp.sin(angles)[:, None, :]
    first = vectors[..., :half]
    second = vectors[..., half:]
    return jnp.concatenate(
        [first * cosine - second * sine, second * cosine + first * sine], axis=-1
    )


def attend_block(
    loop_state, query_matrix, query_pos, query_doc, key_matrix, value_matrix, key_pos, key_doc
):
    best, total, running_output = loop_state
    logit_matrix = jnp.einsum(
        "ucpm,ycm->cpuy", query_matrix, key_matrix, preferred_element_type=jnp.float32
    ) * HEAD_SIZE ** (-0.5)
    allowed = (key_pos[None, :] <= query_pos[:, None]) & (key_doc[None, :] == query_doc[:, None])
    masked = jnp.where(allowed, logit_matrix, jnp.float32(-1e30))
    new_best = jnp.maximum(best, jnp.max(masked, axis=-1))
    correction_scale = jnp.exp(best - new_best)
    attention_weights = jnp.where(
        allowed, jnp.exp(logit_matrix - new_best[..., None]), jnp.float32(0.0)
    )
    total = total * correction_scale + jnp.sum(attention_weights, axis=-1)
    running_output = running_output * correction_scale[..., None] + jnp.einsum(
        "sfec,csh->sfeh",
        attention_weights.astype(jnp.bfloat16),
        value_matrix,
        preferred_element_type=jnp.float32,
    )
    return (new_best, total, running_output)


def shards(hidden, norm_gain, w_query, w_key, w_value, w_out, doc_ids):
    tok_rows = hidden.shape[0]
    half_rows = tok_rows // 2
    width = norm_gain.shape[0]
    group = HEADS // KV_HEADS
    local_kv = w_key.shape[1] // HEAD_SIZE
    query_cols = w_query.shape[1]
    key_cols = w_key.shape[1]
    wide_local = hidden.astype(jnp.float32)
    squares = lax.psum(jnp.sum(wide_local * wide_local, axis=1), "tp")
    inverse_rms = lax.rsqrt(squares / width + epsilon)[:, None]
    piece = lax.all_gather(hidden, "tp", axis=1, tiled=True)
    normed_piece = (piece.astype(jnp.float32) * inverse_rms * norm_gain[None, :]).astype(
        jnp.bfloat16
    )
    projected = jnp.concatenate(
        [
            jnp.dot(normed_piece, w_query, preferred_element_type=jnp.float32),
            jnp.dot(normed_piece, w_key, preferred_element_type=jnp.float32),
            jnp.dot(normed_piece, w_value, preferred_element_type=jnp.float32),
        ],
        axis=1,
    )
    cp_rank = lax.axis_index("cp")
    positions = cp_rank * tok_rows + jnp.arange(tok_rows, dtype=jnp.int32)
    query_raw = projected[:, :query_cols].reshape(tok_rows, local_kv * group, HEAD_SIZE)
    key_raw = projected[:, query_cols : query_cols + key_cols].reshape(
        tok_rows, local_kv, HEAD_SIZE
    )
    query_matrix = (
        rotate(query_raw, positions)
        .astype(jnp.bfloat16)
        .reshape(tok_rows, local_kv, group, HEAD_SIZE)
    )
    keys_flat = rotate(key_raw, positions).astype(jnp.bfloat16).reshape(tok_rows, key_cols)
    values_flat = projected[:, query_cols + key_cols :].astype(jnp.bfloat16)
    query_doc = doc_ids.astype(jnp.float32)
    docs_flat = query_doc.astype(jnp.bfloat16)
    first_queries = query_matrix[:half_rows]
    first_pos = positions[:half_rows]
    first_doc = query_doc[:half_rows]
    second_queries = query_matrix[half_rows:]
    second_doc = query_doc[half_rows:]
    second_start = cp_rank * tok_rows + half_rows
    second_pos = second_start + jnp.arange(half_rows, dtype=jnp.int32)
    last_first = cp_rank * tok_rows + half_rows - 1
    last_second = second_start + half_rows - 1
    init_half = (
        jnp.full((local_kv, group, half_rows), -1e30, jnp.float32),
        jnp.zeros((local_kv, group, half_rows), jnp.float32),
        jnp.zeros((local_kv, group, half_rows, HEAD_SIZE), jnp.float32),
    )
    init = (init_half, init_half)
    key_piece = lax.all_gather(keys_flat, "cp", axis=0, tiled=True)
    value_piece = lax.all_gather(values_flat, "cp", axis=0, tiled=True)
    doc_piece = lax.all_gather(docs_flat, "cp", axis=0, tiled=True)
    count = key_piece.shape[0]

    def inner(index, state):
        first_state, second_state = state
        offset = index * tok_rows
        key_blk = lax.dynamic_slice_in_dim(key_piece, offset, tok_rows, 0).reshape(
            tok_rows, local_kv, HEAD_SIZE
        )
        value_blk = lax.dynamic_slice_in_dim(value_piece, offset, tok_rows, 0).reshape(
            tok_rows, local_kv, HEAD_SIZE
        )
        key_doc = lax.dynamic_slice_in_dim(doc_piece, offset, tok_rows, 0).astype(jnp.float32)
        key_pos = offset + jnp.arange(tok_rows, dtype=jnp.int32)

        def attend_first(inner_state):
            return attend_block(
                inner_state,
                first_queries,
                first_pos,
                first_doc,
                key_blk,
                value_blk,
                key_pos,
                key_doc,
            )

        def attend_second(inner_state):
            return attend_block(
                inner_state,
                second_queries,
                second_pos,
                second_doc,
                key_blk,
                value_blk,
                key_pos,
                key_doc,
            )

        first_state = lax.cond(
            offset <= last_first, attend_first, lambda inner_state: inner_state, first_state
        )
        second_state = lax.cond(
            offset <= last_second, attend_second, lambda inner_state: inner_state, second_state
        )
        return (first_state, second_state)

    final = lax.fori_loop(0, count // tok_rows, inner, init)

    def finish(state):
        result = state[2] / state[1][..., None]
        return (
            jnp.transpose(result, (2, 0, 1, 3)).reshape(half_rows, query_cols).astype(jnp.bfloat16)
        )

    attended_first = finish(final[0])
    attended_second = finish(final[1])
    attended = jnp.concatenate([attended_first, attended_second], axis=0)
    terms = jnp.dot(attended, w_out, preferred_element_type=jnp.float32)
    summed = lax.psum_scatter(terms.astype(jnp.bfloat16), "tp", scatter_dimension=1, tiled=True)
    return summed


def solution(mesh):
    in_specs = (
        P("cp", "tp"),
        P(),
        P(None, "tp"),
        P(None, "tp"),
        P(None, "tp"),
        P("tp", None),
        P("cp"),
    )
    out_specs = P("cp", "tp")
    return jax.shard_map(shards, mesh=mesh, in_specs=in_specs, out_specs=out_specs, check_vma=False)
```

profile of v0, /device:TPU:0, one launch (start us, length us, event | category | flops | bytes accessed | tf_op | source)
XLA Modules:
  0.0 622.3 jit_solution(9094426565222155319)
XLA Ops:
  7.3 2.1 multiply_reduce_fusion
  9.4 5.9 psum.7
  15.8 52.5 %all-gather.5.cloned.1.call-done = bf16[512,4096]{1,0:T(8,128)(2,1)} async-done(((bf16[512,2048]{1,0:T(8,128)(2,1)}), bf16[512,4096]{1,0:T(8,128)(2,1)}) %all-gather.5.cloned.1.call-update) | async-done | bytes 4194320 | tf_op jit(solution)/shard_map/all_gather | solution.py:61
  68.4 5.9 fusion.44
  75.4 6.6 %convolution_convert_fusion.1 = bf16[512,512]{1,0:T(8,128)(2,1)} fusion(bf16[4096,512]{1,0:T(8,128)(2,1)} %param.17, bf16[512,4096]{1,0:T(8,128)(2,1)} %all-gather.5.cloned.1.call-done, f32[4096]{0:T(1024)S(1)} %copy-done.7, f32[512]{0:T(512)S(1)} %add_rsqrt_fusion), kind=kOutput, calls=%fused_computation.61 | convolution fusion | flops 2156134400 | bytes 8931328 | tf_op jit(solution)/shard_map/dot_general | solution.py:69
  82.4 22.4 %all-gather = bf16[16,1,512]{2,1,0:T(2,128)(2,1)S(1)} all-gather(bf16[1,1,512]{2,1,0:T(2,128)(2,1)S(1)} %reshape.106), channel_id=1, replica_groups=mesh['cp'=16,'tp'=2] {'cp'}, dimensions={0}, use_global_device_ids=true | all-gather | bytes 17408 | tf_op jit(solution)/shard_map/all_gather | solution.py:105
  105.0 13.1 %convolution_bitcast_fusion = f32[64,8,16,128]{3,1,2,0:T(8,128)S(1)} fusion(bf16[4096,2048]{1,0:T(8,128)(2,1)} %param.15, bf16[512,4096]{1,0:T(8,128)(2,1)} %all-gather.5.cloned.1.call-done, f32[4096]{0:T(1024)S(1)} %copy-done.7, f32[512]{0:T(512)S(1)} %add_rsqrt_fusion), kind=kOutput, calls=%fused_computation.53 | convolution fusion | flops 8598323200 | bytes 25184256 | tf_op jit(solution)/shard_map/dot_general | solution.py:67
  119.0 1.6 add_convert_fusion
  120.6 1.2 pad_maximum_fusion
  122.3 31.2 %all-gather.7.cloned.1.call-done = bf16[8192,512]{0,1:T(8,128)(2,1)} async-done(((bf16[512,512]{0,1:T(8,128)(2,1)}), bf16[8192,512]{0,1:T(8,128)(2,1)}) %all-gather.7.cloned.1.call-update) | async-done | bytes 8388624 | tf_op jit(solution)/shard_map/all_gather | solution.py:103
  153.5 74.7 %all-gather.9.cloned.1.call-done = bf16[8192,512]{1,0:T(8,128)(2,1)} async-done(((bf16[512,512]{1,0:T(8,128)(2,1)}), bf16[8192,512]{1,0:T(8,128)(2,1)}) %all-gather.9.cloned.1.call-update) | async-done | bytes 8388624 | tf_op jit(solution)/shard_map/all_gather | solution.py:104
  228.2 1.5 broadcast_in_dim.42
  229.7 1.6 broadcast_in_dim.42.clone
  231.3 68.3 %while.24 = (s32[]{:T(128)}, f32[4,4,256]{2,1,0:T(4,128)S(1)}, f32[4,4,256]{2,1,0:T(4,128)S(1)}, f32[4,4,256,128]{3,2,1,0:T(8,128)}, f32[4,4,256]{2,1,0:T(4,128)...) while((s32[]{:T(128)}, f32[4,4,256]{2,1,0:T(4,128)S(1)}, ...), condition=%wide.region_11.12_spmd.clone, body=%wide.region_2.11_spmd.clone.sunk | while | flops 2196522240 | bytes 105403112 | solution.py:152
  231.3 1.1 constant_dynamic-slice_fusion.4
  232.4 1.1 constant_dynamic-slice_fusion.5
  234.5 8.1 %conditional.6 = ((f32[4,4,256]{2,1,0:T(4,128)S(1)}, f32[4,4,256]{2,1,0:T(4,128)S(1)}, f32[4,4,256,128]{3,2,1,0:T(8,128)})) conditional(s32[]{:T(128)} %convert_element_type.128, (f32[4,4,256]{2,1,0:T(4,128)S(1)}, f32[4,4,256]{2,1,0:T(4,128)S(1)}, f32[4,4,256,128]{3,2,1,0:T(8,128)}) %tuple.72, (s32[512]{0:T(512)S(1)}, s32[256]{0:T(256)S(1)}, ...), branch_computations={%region_3.0_spmd, %region_4.6_spmd} | conditional | flops 1098260480 | bytes 51124340 | solution.py:144
  234.7 1.6 fusion.2
  236.3 1.7 fusion.6
  238.1 3.2 multiply_add_fusion
  241.3 1.3 copy-done.3
  242.6 8.1 %conditional.7 = ((f32[4,4,256]{2,1,0:T(4,128)S(1)}, f32[4,4,256]{2,1,0:T(4,128)S(1)}, f32[4,4,256,128]{3,2,1,0:T(8,128)})) conditional(s32[]{:T(128)} %convert_element_type.129, (f32[4,4,256]{2,1,0:T(4,128)S(1)}, f32[4,4,256]{2,1,0:T(4,128)S(1)}, f32[4,4,256,128]{3,2,1,0:T(8,128)}) %tuple.74, (s32[512]{0:T(512)S(1)}, s32[]{:T(128)}, ...), branch_computations={%region_7.7_spmd, %region_8.10_spmd} | conditional | flops 1098260736 | bytes 51126392 | solution.py:147
  242.8 1.6 fusion.20
  244.4 1.7 fusion.24
  246.1 3.2 multiply_add_fusion.2
  249.3 1.3 copy-done.5
  250.7 1.1 constant_dynamic-slice_fusion.4
  251.8 1.1 constant_dynamic-slice_fusion.5
  252.9 1.0 copy.59
  254.0 1.1 constant_dynamic-slice_fusion.4
  255.1 1.1 constant_dynamic-slice_fusion.5
  257.3 1.1 constant_dynamic-slice_fusion.4
  258.3 1.1 constant_dynamic-slice_fusion.5
  260.5 1.1 constant_dynamic-slice_fusion.4
  261.6 1.1 constant_dynamic-slice_fusion.5
  262.7 1.0 copy.59
  263.8 1.1 constant_dynamic-slice_fusion.4
  264.9 1.1 constant_dynamic-slice_fusion.5
  265.9 1.0 copy.59
  267.0 1.1 constant_dynamic-slice_fusion.4
  268.1 1.1 constant_dynamic-slice_fusion.5
  270.3 1.1 constant_dynamic-slice_fusion.4
  271.4 1.1 constant_dynamic-slice_fusion.5
  273.6 1.1 constant_dynamic-slice_fusion.4
  274.6 1.1 constant_dynamic-slice_fusion.5
  276.8 1.1 constant_dynamic-slice_fusion.4
  277.9 1.1 constant_dynamic-slice_fusion.5
  280.1 1.1 constant_dynamic-slice_fusion.4
  281.2 1.1 constant_dynamic-slice_fusion.5
  283.3 1.1 constant_dynamic-slice_fusion.4
  284.4 1.1 constant_dynamic-slice_fusion.5
  286.6 1.1 constant_dynamic-slice_fusion.4
  287.7 1.1 constant_dynamic-slice_fusion.5
  289.9 1.1 constant_dynamic-slice_fusion.4
  290.9 1.1 constant_dynamic-slice_fusion.5
  293.1 1.1 constant_dynamic-slice_fusion.4
  294.2 1.1 constant_dynamic-slice_fusion.5
  296.4 1.1 constant_dynamic-slice_fusion.4
  297.5 1.1 constant_dynamic-slice_fusion.5
  299.6 1.9 copy.40
  301.5 2.9 copy.39
  304.4 2.1 divide_convert_fusion
  306.5 14.0 %convolution_convert_fusion = bf16[512,4096]{1,0:T(8,128)(2,1)} fusion(bf16[2048,4096]{1,0:T(8,128)(2,1)} %param.18, bf16[256,2048]{0,1:T(8,128)(2,1)S(1)} %bitcast.110, bf16[256,2048]{0,1:T(8,128)(2,1)S(1)} %bitcast.111), kind=kOutput, calls=%fused_computation.49 | convolution fusion | flops 8596226048 | bytes 23068672 | tf_op jit(solution)/shard_map/dot_general | solution.py:163
  320.5 295.2 %reduce-scatter.2.cloned.1.call-done = bf16[512,2048]{1,0:T(8,128)(2,1)} async-done(((bf16[512,4096]{1,0:T(8,128)(2,1)}), bf16[512,2048]{1,0:T(8,128)(2,1)}) %reduce-scatter.2.cloned.1.call-update) | async-done | bytes 2097168 | tf_op jit(solution)/shard_map/reduce_scatter | solution.py:164
  (144 shorter events, 19.3 us)
Async XLA Ops:
  6.5 61.8 %copy-start.7 = (f32[4096]{0:T(1024)S(1)}, f32[4096]{0:T(1024)}, u32[]{:S(2)}) copy-start(f32[4096]{0:T(1024)} %param.14) | copy-start | bytes 49156
  6.5 61.8 %all-gather.5.cloned.1.call-start = ((), (), s32[]{:S(2)}) async-start(), calls=%async_computation.1 | async-start | bytes 6291456 | tf_op jit(solution)/shard_map/all_gather | solution.py:61
  7.3 146.2 %all-gather.7.cloned.1.call-start = ((), (), s32[]{:S(2)}) async-start(), calls=%async_computation.2 | async-start | bytes 8912896 | tf_op jit(solution)/shard_map/all_gather | solution.py:103
  75.3 7.0 %copy-start.6 = (s32[512]{0:T(512)S(1)}, s32[512]{0:T(512)}, u32[]{:S(2)}) copy-start(s32[512]{0:T(512)} %param.19) | copy-start | bytes 6148
  75.4 152.8 %all-gather.9.cloned.1.call-start = ((), (), s32[]{:S(2)}) async-start(), calls=%async_computation.3 | async-start | bytes 8912896 | tf_op jit(solution)/shard_map/all_gather | solution.py:104
  82.1 533.7 %reduce-scatter.2.cloned.1.call-start = ((), (), s32[]{:S(2)}) async-start(), calls=%async_computation.4 | async-start | bytes 6291456 | tf_op jit(solution)/shard_map/reduce_scatter | solution.py:164
  236.3 1.8 copy-start
  236.3 1.8 copy-start.2
  241.2 1.3 copy-start.3
  244.4 1.8 copy-start.1
  244.4 1.8 copy-start.4
  249.3 1.3 copy-start.5
Sparse Core Ops, SparseCore 0:
  8.9 59.4 all-gather.4
  75.5 77.9 all-gather.6
  155.6 72.4 all-gather.8
  320.7 295.0 reduce-scatter.1
where the time goes:
time: 625 us; the launch traced here: 622 us
  waiting for transfers between devices  454 us (73%)
  local copies, waits for them, and re-layouts  63.1 us (10%)
  matrix products  49.1 us (8%)
  blocking collectives  28.3 us (5%)
  other arithmetic  13.6 us (2%)
  between operations  13.3 us (2%)
    reduce_scatter x1, waiting for transfers between devices, shards(): lax.psum_scatter(terms.astype(jnp.bfloat16), 'tp', scatter_dimension=1, t...  295 us
    all_gather x1, waiting for transfers between devices, shards(): value_piece = lax.all_gather(values_flat, 'cp', axis=0, tiled=True)  74.7 us
    all_gather x1, waiting for transfers between devices, shards(): piece = lax.all_gather(hidden, 'tp', axis=1, tiled=True)  52.5 us
    dynamic_slice x32, local copies, waits for them, and re-layouts, inner(): lax.dynamic_slice_in_dim(value_piece, offset, tok_rows, 0)  33.5 us
    all_gather x1, waiting for transfers between devices, shards(): key_piece = lax.all_gather(keys_flat, 'cp', axis=0, tiled=True)  31.2 us
    all_gather x1, blocking collectives, shards(): doc_piece = lax.all_gather(docs_flat, 'cp', axis=0, tiled=True)  22.4 us
    dynamic_slice x16, local copies, waits for them, and re-layouts, inner(): lax.dynamic_slice_in_dim(key_piece, offset, tok_rows, 0)  17.2 us
    dot_general x1, matrix products, shards(): terms = jnp.dot(attended, w_out, preferred_element_type=jnp.float32)  14 us
  transfers between devices with their start and end apart: 4, of which 4 were waited for; matrix products, arithmetic and copies ran while one was open for 4% of the time, Pallas kernels for 0%

commit v1 on v0

--- a/solution.py
+++ b/solution.py
@@ -100,8 +100,15 @@
         jnp.zeros((local_kv, group, half_rows, HEAD_SIZE), jnp.float32),
     )
     init = (init_half, init_half)
-    key_piece = lax.all_gather(keys_flat, "cp", axis=0, tiled=True)
-    value_piece = lax.all_gather(values_flat, "cp", axis=0, tiled=True)
+
+    def clusters_store(xx, xin):
+        return jnp.split(
+            lax.all_gather(jnp.concatenate([xx, xin], 1), axis_name="cp", axis=0, tiled=True),
+            [xx.shape[1]],
+            1,
+        )
+
+    key_piece, value_piece = clusters_store(keys_flat, values_flat)
     doc_piece = lax.all_gather(docs_flat, "cp", axis=0, tiled=True)
     count = key_piece.shape[0]
 

time: 625 us -> 583 us (0.933)
  local copies, waits for them, and re-layouts: 63.1 us -> 44.3 us
  waiting for transfers between devices: 454 us -> 436 us
    dynamic_slice x16 -> x0, local copies, waits for them, and re-layouts: 17.2 us -> none  [inner(): lax.dynamic_slice_in_dim(key_piece, offset, tok_rows, 0)]
    all_gather x2 -> x1, waiting for transfers between devices: 106 us -> 90.2 us  [clusters_store(): lax.all_gather(jnp.concatenate([xx, xin], 1), axis_name='cp', axis=0, til...]
    dynamic_slice x32 -> x16, local copies, waits for them, and re-layouts: 33.5 us -> 20.4 us  [inner(): lax.dynamic_slice_in_dim(value_piece, offset, tok_rows, 0)]
    split x0 -> x1, local copies, waits for them, and re-layouts: none -> 11.5 us  [clusters_store(): jnp.split(lax.all_gather(jnp.concatenate([xx, xin], 1), axis_name='cp', a...]
  transfers between devices with their start and end apart: 4 -> 3, of which waited for: 4 -> 3; matrix products, arithmetic and copies ran while one was open for 4% -> 3% of each run, Pallas kernels for 0% -> 0%
where the time goes in v1:
time: 583 us
  waiting for transfers between devices  436 us (75%)
  matrix products  45.3 us (8%)
  local copies, waits for them, and re-layouts  44.3 us (8%)
  blocking collectives  28 us (5%)
  other arithmetic  14 us (2%)
  between operations  13.3 us (2%)
    reduce_scatter x1, waiting for transfers between devices, shards(): lax.psum_scatter(terms.astype(jnp.bfloat16), 'tp', scatter_dimension=1, t...  293 us
    all_gather x1, waiting for transfers between devices, clusters_store(): lax.all_gather(jnp.concatenate([xx, xin], 1), axis_name='cp', axis=0, til...  90.2 us
    all_gather x1, waiting for transfers between devices, shards(): piece = lax.all_gather(hidden, 'tp', axis=1, tiled=True)  52.5 us
    all_gather x1, blocking collectives, shards(): doc_piece = lax.all_gather(docs_flat, 'cp', axis=0, tiled=True)  22.1 us
    dynamic_slice x16, local copies, waits for them, and re-layouts, inner(): lax.dynamic_slice_in_dim(value_piece, offset, tok_rows, 0)  20.4 us
    dot_general x1, matrix products, shards(): terms = jnp.dot(attended, w_out, preferred_element_type=jnp.float32)  14 us
    dot_general x1, matrix products, shards(): jnp.dot(normed_piece, w_query, preferred_element_type=jnp.float32)  13.1 us
  transfers between devices with their start and end apart: 3, of which 3 were waited for; matrix products, arithmetic and copies ran while one was open for 3% of the time, Pallas kernels for 0%

profile of v1, /device:TPU:0, one launch (start us, length us, event | category | flops | bytes accessed | tf_op | source)
XLA Modules:
  0.0 582.8 jit_solution(12041520822038819065)
XLA Ops:
  6.5 0.7 all-gather.4.cloned.1.call-update
  7.3 2.1 multiply_reduce_fusion
  9.4 5.9 %psum.7 = f32[512]{0:T(512)S(1)} all-reduce(f32[512]{0:T(512)S(1)} %multiply_reduce_fusion), channel_id=1, replica_groups=mesh['cp'=16,'tp'=2] {'tp'}, use_global_device_ids=true, to_apply=%region_1.0 | all-reduce | flops 512 | bytes 4096 | tf_op jit(solution)/shard_map/psum | solution.py:59
  15.3 0.5 multiply_cosine_fusion
  15.8 52.5 %all-gather.4.cloned.1.call-done = bf16[512,4096]{1,0:T(8,128)(2,1)} async-done(((bf16[512,2048]{1,0:T(8,128)(2,1)}), bf16[512,4096]{1,0:T(8,128)(2,1)}) %all-gather.4.cloned.1.call-update) | async-done | bytes 4194320 | tf_op jit(solution)/shard_map/all_gather | solution.py:61
  68.4 6.1 %fusion.44 = f32[512,512]{0,1:T(8,128)S(1)} fusion(bf16[4096,512]{1,0:T(8,128)(2,1)} %param.16, bf16[512,4096]{1,0:T(8,128)(2,1)} %all-gather.4.cloned.1.call-done, f32[4096]{0:T(1024)S(1)} %copy-done.7, f32[512]{0:T(512)S(1)} %add_rsqrt_fusion), kind=kOutput, calls=%fused_computation.76 | convolution fusion | flops 2155872256 | bytes 9455616 | tf_op jit(solution)/shard_map/dot_general | solution.py:68
  74.4 0.2 subtract_convert_fusion.1
  74.7 2.6 convolution_convert_fusion.1
  77.3 1.0 pad_maximum_fusion.1
  78.4 0.1 copy.34
  78.6 0.1 copy.35
  78.7 22.1 %all-gather = bf16[16,1,512]{2,1,0:T(2,128)(2,1)S(1)} all-gather(bf16[1,1,512]{2,1,0:T(2,128)(2,1)S(1)} %reshape.106), channel_id=1, replica_groups=mesh['cp'=16,'tp'=2] {'cp'}, dimensions={0}, use_global_device_ids=true | all-gather | bytes 17408 | tf_op jit(solution)/shard_map/all_gather | solution.py:112
  100.8 0.1 reduce
  101.0 13.1 %convolution_bitcast_fusion = f32[64,8,16,128]{3,1,2,0:T(8,128)S(1)} fusion(bf16[4096,2048]{1,0:T(8,128)(2,1)} %param.15, bf16[512,4096]{1,0:T(8,128)(2,1)} %all-gather.4.cloned.1.call-done, f32[4096]{0:T(1024)S(1)} %copy-done.7, f32[512]{0:T(512)S(1)} %add_rsqrt_fusion), kind=kOutput, calls=%fused_computation.53 | convolution fusion | flops 8598323200 | bytes 25184256 | tf_op jit(solution)/shard_map/dot_general | solution.py:67
  114.1 0.9 copy.55
  115.0 1.6 add_convert_fusion
  116.6 1.2 pad_maximum_fusion
  117.8 0.3 copy.37
  118.0 0.3 copy.36
  118.3 90.2 %all-gather.6.cloned.1.call-done = bf16[8192,1024]{0,1:T(8,128)(2,1)} async-done(((bf16[512,1024]{0,1:T(8,128)(2,1)}), bf16[8192,1024]{0,1:T(8,128)(2,1)}) %all-gather.6.cloned.1.call-update) | async-done | bytes 16777232 | tf_op jit(solution)/shard_map/all_gather | solution.py:106
  208.5 11.5 %fusion.45 = (bf16[8192,512]{0,1:T(8,128)(2,1)}, bf16[8192,512]{0,1:T(8,128)(2,1)}) fusion(bf16[8192,1024]{0,1:T(8,128)(2,1)} %all-gather.6.cloned.1.call-done), kind=kLoop, calls=%fused_computation.77 | loop fusion | bytes 33554432 | tf_op jit(solution)/shard_map/split | solution.py:105
  220.1 1.5 broadcast_in_dim.42.clone
  221.6 1.5 broadcast_in_dim.42
  223.2 39.6 %while.24 = (s32[]{:T(128)}, f32[4,4,256]{2,1,0:T(4,128)S(1)}, f32[4,4,256]{2,1,0:T(4,128)S(1)}, f32[4,4,256,128]{3,2,1,0:T(8,128)}, f32[4,4,256]{2,1,0:T(4,128)...) while((s32[]{:T(128)}, f32[4,4,256]{2,1,0:T(4,128)S(1)}, ...), condition=%wide.region_11.12_spmd.clone, body=%wide.region_2.11_spmd.clone.sunk | while | flops 2196522240 | bytes 100160168 | solution.py:159
  223.3 1.3 constant_dynamic-slice_fusion.3
  224.5 8.1 %conditional.7 = ((f32[4,4,256]{2,1,0:T(4,128)S(1)}, f32[4,4,256]{2,1,0:T(4,128)S(1)}, f32[4,4,256,128]{3,2,1,0:T(8,128)})) conditional(s32[]{:T(128)} %convert_element_type.129, (f32[4,4,256]{2,1,0:T(4,128)S(1)}, f32[4,4,256]{2,1,0:T(4,128)S(1)}, f32[4,4,256,128]{3,2,1,0:T(8,128)}) %tuple.77, (s32[512]{0:T(512)S(1)}, s32[]{:T(128)}, ...), branch_computations={%region_7.7_spmd, %region_8.10_spmd} | conditional | flops 1098260736 | bytes 49029212 | solution.py:154
  224.6 0.2 compare_and_fusion.1
  224.8 1.5 fusion.20
  226.4 1.7 fusion.24
  228.1 3.2 multiply_add_fusion.2
  231.3 1.3 copy-done.1
  232.6 8.0 %conditional.6 = ((f32[4,4,256]{2,1,0:T(4,128)S(1)}, f32[4,4,256]{2,1,0:T(4,128)S(1)}, f32[4,4,256,128]{3,2,1,0:T(8,128)})) conditional(s32[]{:T(128)} %convert_element_type.128, (f32[4,4,256]{2,1,0:T(4,128)S(1)}, f32[4,4,256]{2,1,0:T(4,128)S(1)}, f32[4,4,256,128]{3,2,1,0:T(8,128)}) %tuple.75, (s32[512]{0:T(512)S(1)}, s32[256]{0:T(256)S(1)}, ...), branch_computations={%region_3.0_spmd, %region_4.6_spmd} | conditional | flops 1098260480 | bytes 49027160 | solution.py:151
  232.6 0.2 compare_and_fusion
  232.8 1.6 fusion.2
  234.4 1.7 fusion.6
  236.1 3.2 multiply_add_fusion
  239.3 1.3 copy-done.3
  240.7 0.1 dynamic-slice_convert_fusion.2
  240.7 1.3 constant_dynamic-slice_fusion.3
  242.1 0.1 dynamic-slice_convert_fusion.2
  242.2 1.3 constant_dynamic-slice_fusion.3
  243.6 0.1 dynamic-slice_convert_fusion.2
  243.7 1.3 constant_dynamic-slice_fusion.3
  245.0 0.1 dynamic-slice_convert_fusion.2
  245.1 1.3 constant_dynamic-slice_fusion.3
  246.5 0.1 dynamic-slice_convert_fusion.2
  246.6 1.3 constant_dynamic-slice_fusion.3
  248.0 0.1 dynamic-slice_convert_fusion.2
  248.1 1.3 constant_dynamic-slice_fusion.3
  249.4 0.1 dynamic-slice_convert_fusion.2
  249.5 1.3 constant_dynamic-slice_fusion.3
  251.0 1.3 constant_dynamic-slice_fusion.3
  252.4 1.3 constant_dynamic-slice_fusion.3
  253.9 1.3 constant_dynamic-slice_fusion.3
  255.4 1.3 constant_dynamic-slice_fusion.3
  256.8 1.3 constant_dynamic-slice_fusion.3
  258.3 1.3 constant_dynamic-slice_fusion.3
  259.7 1.3 constant_dynamic-slice_fusion.3
  261.2 1.3 constant_dynamic-slice_fusion.3
  262.8 1.9 copy.39
  264.7 2.9 copy.38
  267.6 2.1 divide_convert_fusion
  269.7 14.0 %convolution_convert_fusion = bf16[512,4096]{1,0:T(8,128)(2,1)} fusion(bf16[2048,4096]{1,0:T(8,128)(2,1)} %param.18, bf16[256,2048]{0,1:T(8,128)(2,1)S(1)} %bitcast.110, bf16[256,2048]{0,1:T(8,128)(2,1)S(1)} %bitcast.111), kind=kOutput, calls=%fused_computation.49 | convolution fusion | flops 8596226048 | bytes 23068672 | tf_op jit(solution)/shard_map/dot_general | solution.py:170
  283.7 292.5 %reduce-scatter.2.cloned.1.call-done = bf16[512,2048]{1,0:T(8,128)(2,1)} async-done(((bf16[512,4096]{1,0:T(8,128)(2,1)}), bf16[512,2048]{1,0:T(8,128)(2,1)}) %reduce-scatter.2.cloned.1.call-update) | async-done | bytes 2097168 | tf_op jit(solution)/shard_map/reduce_scatter | solution.py:171
  (111 shorter events, 1.6 us)
Async XLA Ops:
  6.5 61.8 %copy-start.7 = (f32[4096]{0:T(1024)S(1)}, f32[4096]{0:T(1024)}, u32[]{:S(2)}) copy-start(f32[4096]{0:T(1024)} %param.14) | copy-start | bytes 49156
  6.5 61.8 %all-gather.4.cloned.1.call-start = ((), (), s32[]{:S(2)}) async-start(), calls=%async_computation.1 | async-start | bytes 6291456 | tf_op jit(solution)/shard_map/all_gather | solution.py:61
  7.3 201.3 %all-gather.6.cloned.1.call-start = ((), (), s32[]{:S(2)}) async-start(), calls=%async_computation.2 | async-start | bytes 17825792 | tf_op jit(solution)/shard_map/all_gather | solution.py:106
  68.4 6.3 %copy-start.5 = (bf16[4096,512]{1,0:T(8,128)(2,1)S(1)}, bf16[4096,512]{1,0:T(8,128)(2,1)}, u32[]{:S(2)}) copy-start(bf16[4096,512]{1,0:T(8,128)(2,1)} %param.17) | copy-start | bytes 12582916
  68.4 6.3 %copy-start.6 = (bf16[512,4096]{1,0:T(8,128)(2,1)S(1)}, bf16[512,4096]{1,0:T(8,128)(2,1)}, u32[]{:S(2)}) copy-start(bf16[512,4096]{1,0:T(8,128)(2,1)} %all-gather.4.cloned.1.call-done) | copy-start | bytes 12582916
  74.7 4.0 copy-start.4
  78.4 497.9 %reduce-scatter.2.cloned.1.call-start = ((), (), s32[]{:S(2)}) async-start(), calls=%async_computation.3 | async-start | bytes 6291456 | tf_op jit(solution)/shard_map/reduce_scatter | solution.py:171
  226.4 1.7 copy-start
  231.3 1.3 copy-start.1
  234.4 1.7 copy-start.2
  239.3 1.3 copy-start.3
Sparse Core Ops, SparseCore 0:
  8.9 59.4 all-gather.3
  78.5 129.9 all-gather.5
  283.9 292.3 reduce-scatter.1
